TPU v7x, 32 devices: a whole 2x2x4 slice. The times are simulated.
32 devices in a mesh: batch: 4 (over y, core), tensor: 2 (over x), latent: 4 (over z).
Axes of the slice: x: 2, y: 2, z: 4, core: 2. Of those that a mesh axis runs over, the one named last changes fastest.
Arguments:
- residual: bfloat16 [1024, 3584], P('batch', ('tensor', 'latent')), may hold values from -6 to 6
- target: bfloat16 [1024, 3584], P('batch', ('tensor', 'latent')), may hold values from -6 to 6
- encoder_weight: bfloat16 [3584, 32768], P(None, ('tensor', 'latent')), may hold values from -0.09375 to 0.09375
- encoder_bias: bfloat16 [32768], P(('tensor', 'latent')), may hold values from -0.59765625 to 0.29882812
- decoder_weight: bfloat16 [32768, 3584], P(('tensor', 'latent')), may hold values from -0.0625 to 0.0625
- decoder_bias: bfloat16 [3584], replicated, may hold values from -3 to 3
- first_gain: bfloat16 [3584], replicated, may hold values from 0.5 to 1.5
- second_gain: bfloat16 [3584], replicated, may hold values from 0.5 to 1.5
- gate_weight: bfloat16 [3584, 7168], P(None, ('tensor', 'latent')), may hold values from -0.09375 to 0.09375
- up_weight: bfloat16 [3584, 7168], P(None, ('tensor', 'latent')), may hold values from -0.09375 to 0.09375
- down_weight: bfloat16 [7168, 3584], P(('tensor', 'latent')), may hold values from -0.09375 to 0.09375
Outputs:
- encoder_grad: bfloat16 [3584, 32768], P('batch', ('tensor', 'latent'))
- decoder_grad: bfloat16 [32768, 3584], P(('tensor', 'latent'), 'batch')
All inputs are finite; a program needn't handle non-finite values.
Results may differ from a plain program's by a relative error of at most 0.012.
The roundings to bfloat16 on the way count: a program that leaves them out, or rounds other values in their place, can miss the bound.
Values may be sent and summed in bfloat16 or wider, within the bound.
A program may use at most 192 MiB of HBM per device.

v0:
```python
import jax
import jax.numpy as jnp
from jax import lax
from jax.sharding import PartitionSpec as P

epsilon = 1e-06


def per_device(
    residual,
    target,
    encoder_weight,
    encoder_bias,
    decoder_weight,
    decoder_bias,
    first_gain,
    second_gain,
    gate_weight,
    up_weight,
    down_weight,
):
    f32 = jnp.float32
    bf16 = jnp.bfloat16
    contract_last = (((1,), (1,)), ((), ()))
    contract_first = (((0,), (0,)), ((), ()))
    share_width = residual.shape[1]
    model_width = share_width * lax.axis_size(("tensor", "latent"))
    offset = lax.axis_index(("tensor", "latent")) * share_width
    token_count = residual.shape[0] * lax.axis_size("batch")
    bias_share = lax.dynamic_slice_in_dim(decoder_bias.astype(f32), offset, share_width)
    first_share = lax.dynamic_slice_in_dim(first_gain.astype(f32), offset, share_width)
    second_share = lax.dynamic_slice_in_dim(second_gain.astype(f32), offset, share_width)
    centered_share = (residual.astype(f32) - bias_share).astype(bf16)
    centered = lax.all_gather(centered_share, ("tensor", "latent"), axis=1, tiled=True)
    preact = jnp.dot(centered, encoder_weight, preferred_element_type=f32) + encoder_bias.astype(
        f32
    )
    latents = jnp.maximum(preact, 0.0).astype(bf16)
    partial_recon = jnp.dot(latents, decoder_weight, preferred_element_type=f32)
    recon_full = lax.psum(partial_recon.astype(jnp.bfloat16), ("tensor", "latent")).astype(
        jnp.float32
    ) + decoder_bias.astype(f32)
    scale_in = lax.rsqrt(
        jnp.sum(recon_full * recon_full, axis=1, keepdims=True) / model_width + epsilon
    )
    normed_input = (recon_full * scale_in * first_gain.astype(f32)).astype(bf16)
    recon = lax.dynamic_slice_in_dim(recon_full, offset, share_width, 1)
    gate_value = jnp.dot(normed_input, gate_weight, preferred_element_type=f32)
    up_value = jnp.dot(normed_input, up_weight, preferred_element_type=f32)
    gelu_value, gelu_back = jax.vjp(lambda v: jax.nn.gelu(v, approximate=True), gate_value)
    hidden = (gelu_value * up_value).astype(bf16)
    partial_out = jnp.dot(hidden, down_weight, preferred_element_type=f32)
    output = lax.psum_scatter(
        partial_out.astype(jnp.bfloat16), ("tensor", "latent"), scatter_dimension=1, tiled=True
    ).astype(jnp.float32)
    out_squares = lax.psum(jnp.sum(output * output, axis=1), ("tensor", "latent"))
    scale_out = lax.rsqrt(out_squares[:, None] / model_width + epsilon)
    normed_out = output * scale_out
    result = recon + normed_out * second_share
    grad_result = 2.0 * (result - target.astype(f32)) / token_count
    grad_normed = grad_result * second_share
    inner_out = (
        lax.psum(jnp.sum(grad_normed * normed_out, axis=1), ("tensor", "latent")) / model_width
    )
    grad_share = (scale_out * (grad_normed - normed_out * inner_out[:, None])).astype(bf16)
    grad_output = lax.all_gather(grad_share, ("tensor", "latent"), axis=1, tiled=True)
    grad_hidden = lax.dot_general(
        grad_output, down_weight, contract_last, preferred_element_type=f32
    )
    grad_gate = gelu_back(grad_hidden * up_value)[0].astype(bf16)
    grad_up = (grad_hidden * gelu_value).astype(bf16)
    partial_input = lax.dot_general(
        grad_gate, gate_weight, contract_last, preferred_element_type=f32
    )
    partial_input = partial_input + lax.dot_general(
        grad_up, up_weight, contract_last, preferred_element_type=f32
    )
    grad_normed_in = lax.psum_scatter(
        partial_input.astype(jnp.bfloat16), ("tensor", "latent"), scatter_dimension=1, tiled=True
    ).astype(jnp.float32)
    unit = recon * scale_in
    grad_unit = grad_normed_in * first_share
    inner_in = lax.psum(jnp.sum(grad_unit * unit, axis=1), ("tensor", "latent")) / model_width
    recon_share = (grad_result + scale_in * (grad_unit - unit * inner_in[:, None])).astype(bf16)
    grad_recon = lax.all_gather(recon_share, ("tensor", "latent"), axis=1, tiled=True)
    grad_latent = lax.dot_general(
        grad_recon, decoder_weight, contract_last, preferred_element_type=f32
    )
    grad_preact = jnp.where(preact > 0, grad_latent, 0.0).astype(bf16)
    centered_block, recon_block = (
        lax.all_to_all(centered, "batch", split_axis=1, concat_axis=0, tiled=True),
        lax.all_to_all(grad_recon, "batch", split_axis=1, concat_axis=0, tiled=True),
    )
    latents_all, preact_all = (
        lax.all_gather(latents, "batch", axis=0, tiled=True),
        lax.all_gather(grad_preact, "batch", axis=0, tiled=True),
    )
    encoder_grad = lax.dot_general(
        centered_block, preact_all, contract_first, preferred_element_type=f32
    )
    decoder_grad = lax.dot_general(
        latents_all, recon_block, contract_first, preferred_element_type=f32
    )
    return (encoder_grad.astype(bf16), decoder_grad.astype(bf16))


def solution(mesh):
    in_specs = (
        P("batch", ("tensor", "latent")),
        P("batch", ("tensor", "latent")),
        P(None, ("tensor", "latent")),
        P(("tensor", "latent")),
        P(("tensor", "latent"), None),
        P(),
        P(),
        P(),
        P(None, ("tensor", "latent")),
        P(None, ("tensor", "latent")),
        P(("tensor", "latent"), None),
    )
    out_specs = (P("batch", ("tensor", "latent")), P(("tensor", "latent"), "batch"))
    return jax.shard_map(
        per_device, mesh=mesh, in_specs=in_specs, out_specs=out_specs, check_vma=False
    )
```

profile of v0, /device:TPU:0, one launch (start us, length us, event | category | flops | bytes accessed | tf_op | source)
XLA Modules:
  0.0 670.3 jit_solution(1007464066563289429)
XLA Ops:
  7.2 0.0 all-gather.6.cloned.1.call-start
  7.2 0.8 dynamic_slice.12
  8.0 1.8 subtract_convert_fusion
  9.7 0.0 all-gather.6.cloned.1.call-update
  9.8 0.0 all-reduce.2.cloned.1.call-start
  9.8 0.7 convert_element_type.74
  10.5 49.3 %all-gather.6.cloned.1.call-done = bf16[256,3584]{0,1:T(8,128)(2,1)} async-done(((bf16[256,448]{0,1:T(8,128)(2,1)}), bf16[256,3584]{0,1:T(8,128)(2,1)}) %all-gather.6.cloned.1.call-update) | async-done | bytes 1835024 | tf_op jit(solution)/shard_map/all_gather | solution.py:34
  59.8 15.2 %maximum_convert_fusion = (bf16[256,4096]{1,0:T(8,128)(2,1)S(1)}, f32[256,4096]{1,0:T(8,128)}) fusion(f32[4096]{0:T(1024)S(1)} %convert_element_type.74, bf16[256,3584]{0,1:T(8,128)(2,1)} %all-gather.6.cloned.1.call-done, bf16[3584,4096]{1,0:T(8,128)(2,1)} %param.13), kind=kOutput, calls=%fused_computation.11 | convolution fusion | flops 7519338496 | bytes 37502976 | tf_op jit(solution)/shard_map/dot_general | solution.py:35
  75.0 15.5 %convolution_convert_fusion.2 = bf16[256,3584]{1,0:T(8,128)(2,1)} fusion(bf16[256,4096]{1,0:T(8,128)(2,1)S(1)} %get-tuple-element.4, bf16[4096,3584]{1,0:T(8,128)(2,1)} %param.15), kind=kOutput, calls=%fused_computation.5 | convolution fusion | flops 7517110272 | bytes 33292288 | tf_op jit(solution)/shard_map/dot_general | solution.py:39
  90.4 0.0 copy-done
  90.5 0.0 all-reduce.2.cloned.1.call-update
  90.5 0.2 reduce-scatter.7.cloned.1.call-start
  90.7 94.5 %all-reduce.2.cloned.1.call-done = bf16[256,3584]{1,0:T(8,128)(2,1)} async-done(((bf16[256,3584]{1,0:T(8,128)(2,1)}), bf16[256,3584]{1,0:T(8,128)(2,1)}) %all-reduce.2.cloned.1.call-update) | async-done | bytes 1835024 | tf_op jit(solution)/shard_map/psum | solution.py:40
  185.2 4.0 convert_add_fusion
  189.2 0.0 slice-start.4
  189.2 5.6 fusion.30
  194.9 0.0 slice-start.5
  194.9 2.1 fusion.29
  197.1 0.0 copy-start.4
  197.1 4.3 fusion.2
  201.4 0.0 reduce-scatter.7.cloned.1.call-update
  201.4 0.0 all-gather.8.cloned.1.call-start
  201.4 0.1 copy.36
  201.6 0.8 broadcast_multiply_fusion
  202.4 0.8 dynamic-slice_convert_fusion
  203.1 64.5 %reduce-scatter.7.cloned.1.call-done = bf16[448,256]{1,0:T(8,128)(2,1)} async-done(((bf16[3584,256]{1,0:T(8,128)(2,1)}), bf16[448,256]{1,0:T(8,128)(2,1)}) %reduce-scatter.7.cloned.1.call-update) | async-done | bytes 229392
  267.7 1.1 copy.42
  268.7 0.1 fusion.20
  268.9 19.4 %psum.29 = f32[256]{0:T(256)S(1)} all-reduce(f32[256]{0:T(256)S(1)} %fusion.20), channel_id=1, replica_groups=mesh['batch'=4,'tensor'=2,'latent'=4] {'tensor','latent'}, use_global_device_ids=true, to_apply=%region_4.0 | all-reduce | flops 256 | bytes 2048 | tf_op jit(solution)/shard_map/psum | solution.py:56
  288.3 1.4 fusion.16
  289.7 17.2 %psum.30 = f32[256]{0:T(256)S(1)} all-reduce(f32[256]{0:T(256)S(1)} %fusion.16), channel_id=1, replica_groups=mesh['batch'=4,'tensor'=2,'latent'=4] {'tensor','latent'}, use_global_device_ids=true, to_apply=%region_6.0 | all-reduce | flops 256 | bytes 2048 | tf_op jit(solution)/shard_map/psum | solution.py:63
  307.0 1.4 fusion.19
  308.4 0.9 copy.37
  309.2 0.0 all-gather.8.cloned.1.call-update
  309.2 0.3 reduce-scatter.9.cloned.1.call-start
  309.5 45.8 %all-gather.8.cloned.1.call-done = bf16[256,3584]{0,1:T(8,128)(2,1)} async-done(((bf16[256,448]{0,1:T(8,128)(2,1)}), bf16[256,3584]{0,1:T(8,128)(2,1)}) %all-gather.8.cloned.1.call-update) | async-done | bytes 1835024 | tf_op jit(solution)/shard_map/all_gather | solution.py:66
  355.3 5.6 fusion.45
  361.0 0.0 slice-start.3
  361.0 5.4 fusion.21
  366.5 3.6 fusion.3
  370.1 0.0 reduce-scatter.9.cloned.1.call-update
  370.1 0.0 all-gather.10.cloned.1.call-start
  370.2 0.1 dynamic_slice.15
  370.3 65.2 %reduce-scatter.9.cloned.1.call-done = bf16[448,256]{1,0:T(8,128)(2,1)} async-done(((bf16[3584,256]{1,0:T(8,128)(2,1)}), bf16[448,256]{1,0:T(8,128)(2,1)}) %reduce-scatter.9.cloned.1.call-update) | async-done | bytes 229392
  435.5 1.1 copy.44
  436.6 1.4 multiply_reduce_fusion.1
  438.0 19.3 %psum.31 = f32[256]{0:T(256)S(1)} all-reduce(f32[256]{0:T(256)S(1)} %multiply_reduce_fusion.1), channel_id=1, replica_groups=mesh['batch'=4,'tensor'=2,'latent'=4] {'tensor','latent'}, use_global_device_ids=true, to_apply=%region_9.0 | all-reduce | flops 256 | bytes 2048 | tf_op jit(solution)/shard_map/psum | solution.py:83
  457.3 1.5 add_convert_fusion
  458.8 0.8 copy.39
  459.7 0.0 all-gather.10.cloned.1.call-update
  459.7 0.0 all-gather.14.cloned.1.call-start
  459.7 0.7 all-gather.14.cloned.1.call-update
  460.4 0.0 all-gather.12.cloned.1.call-start
  460.5 44.0 %all-gather.10.cloned.1.call-done = bf16[256,3584]{0,1:T(8,128)(2,1)} async-done(((bf16[256,448]{0,1:T(8,128)(2,1)}), bf16[256,3584]{0,1:T(8,128)(2,1)}) %all-gather.10.cloned.1.call-update) | async-done | bytes 1835024 | tf_op jit(solution)/shard_map/all_gather | solution.py:85
  504.5 18.3 %fusion = bf16[256,4096]{1,0:T(8,128)(2,1)} fusion(bf16[256,3584]{0,1:T(8,128)(2,1)} %all-gather.10.cloned.1.call-done, bf16[4096,3584]{1,0:T(8,128)(2,1)} %param.15, f32[256,4096]{1,0:T(8,128)} %get-tuple-element.5), kind=kOutput, calls=%fused_computation.6 | convolution fusion | flops 7519338496 | bytes 37486592 | tf_op jit(solution)/shard_map/dot_general | solution.py:86
  522.8 0.0 all-gather.12.cloned.1.call-update
  522.8 46.2 %all_to_all.38 = bf16[256,4,896]{0,2,1:T(8,128)(2,1)} all-to-all(bf16[256,4,896]{0,2,1:T(8,128)(2,1)S(1)} %bitcast.35), channel_id=1, replica_groups=mesh['batch'=4,'tensor'=2,'latent'=4] {'batch'}, dimensions={1} | all-to-all | bytes 3670016 | tf_op jit(solution)/shard_map/all_to_all | solution.py:91
  569.0 3.8 all-to-all-start.1
  572.9 3.6 copy.34
  576.5 24.1 %all-to-all-done.1 = bf16[256,4,896]{0,2,1:T(8,128)(2,1)S(1)} async-done(((bf16[256,4,896]{0,2,1:T(8,128)(2,1)}), bf16[256,4,896]{0,2,1:T(8,128)(2,1)S(1)}, u32[]{:S(2)}, u32[]{:S(2)}) %all-to-all-start.1) | async-done | bytes 1835040 | tf_op jit(solution)/shard_map/all_to_all | solution.py:92
  600.6 2.4 copy.40
  603.0 15.2 %convolution_convert_fusion = bf16[4096,896]{1,0:T(8,128)(2,1)} fusion(bf16[1024,4096]{1,0:T(8,128)(2,1)} %all-gather.14.cloned.1.call-done, bf16[1024,896]{1,0:T(8,128)(2,1)} %bitcast.38), kind=kOutput, calls=%fused_computation | convolution fusion | flops 7519862784 | bytes 17563648 | tf_op jit(solution)/shard_map/dot_general | solution.py:101
  618.1 33.3 %all-gather.12.cloned.1.call-done = bf16[1024,4096]{1,0:T(8,128)(2,1)} async-done(((bf16[256,4096]{1,0:T(8,128)(2,1)}), bf16[1024,4096]{1,0:T(8,128)(2,1)}) %all-gather.12.cloned.1.call-update) | async-done | bytes 8388624 | tf_op jit(solution)/shard_map/all_gather | solution.py:96
  651.4 12.1 %convolution_convert_fusion.1 = bf16[896,4096]{1,0:T(8,128)(2,1)} fusion(bf16[1024,896]{1,0:T(8,128)(2,1)S(1)} %bitcast.37, bf16[1024,4096]{1,0:T(8,128)(2,1)} %all-gather.12.cloned.1.call-done), kind=kOutput, calls=%fused_computation.1 | convolution fusion | flops 7519862784 | bytes 17563648 | tf_op jit(solution)/shard_map/dot_general | solution.py:98
  (31 shorter events, 0.1 us)
Async XLA Ops:
  7.2 52.6 %all-gather.6.cloned.1.call-start = ((), (), s32[]{:S(2)}) async-start(), calls=%async_computation.4 | async-start | bytes 2064384 | tf_op jit(solution)/shard_map/all_gather | solution.py:34
  9.8 175.5 %all-reduce.2.cloned.1.call-start = ((), (), s32[]{:S(2)}) async-start(), calls=%async_computation.5 | async-start | bytes 3670016 | tf_op jit(solution)/shard_map/psum | solution.py:40
  75.0 15.5 %copy-start = (bf16[256,4096]{1,0:T(8,128)(2,1)}, bf16[256,4096]{1,0:T(8,128)(2,1)S(1)}, u32[]{:S(2)}) copy-start(bf16[256,4096]{1,0:T(8,128)(2,1)S(1)} %get-tuple-element.4) | copy-start | bytes 6291460
  75.0 15.8 %copy-start.5 = (bf16[3584]{0:T(1024)(128)(2,1)S(1)}, bf16[3584]{0:T(1024)(128)(2,1)}, u32[]{:S(2)}) copy-start(bf16[3584]{0:T(1024)(128)(2,1)} %param.16) | copy-start | bytes 21508
  75.0 15.8 %copy-start.6 = (bf16[3584]{0:T(1024)(128)(2,1)S(1)}, bf16[3584]{0:T(1024)(128)(2,1)}, u32[]{:S(2)}) copy-start(bf16[3584]{0:T(1024)(128)(2,1)} %param.17) | copy-start | bytes 21508
  90.5 177.2 %reduce-scatter.7.cloned.1.call-start = ((), (), s32[]{:S(2)}) async-start(), calls=%async_computation.10 | async-start | bytes 2064384
  185.2 9.6 %slice-start = ((s8[6422528]{0:T(1024)(128)(4,1)}), s8[4194304]{0:T(1024)(128)(4,1)S(1)}, s32[]{:S(2)}) async-start(s8[6422528]{0:T(1024)(128)(4,1)} %bitcast.29), calls=%async_computation.12 | async-start | bytes 8388608
  189.2 5.7 slice-start.1
  189.2 5.7 copy-start.3
  189.2 7.9 %slice-start.4 = ((s8[6422528]{0:T(1024)(128)(4,1)}), s8[4194304]{0:T(1024)(128)(4,1)S(1)}, s32[]{:S(2)}) async-start(s8[6422528]{0:T(1024)(128)(4,1)} %bitcast.41), calls=%async_computation.16 | async-start | bytes 8388608
  194.9 2.2 slice-start.5
  197.1 4.4 copy-start.4
  201.4 154.0 %all-gather.8.cloned.1.call-start = ((), (), s32[]{:S(2)}) async-start(), calls=%async_computation.6 | async-start | bytes 2064384 | tf_op jit(solution)/shard_map/all_gather | solution.py:66
  309.2 126.3 %reduce-scatter.9.cloned.1.call-start = ((), (), s32[]{:S(2)}) async-start(), calls=%async_computation.11 | async-start | bytes 2064384
  355.3 11.1 %slice-start.2 = ((s8[6422528]{0:T(1024)(128)(4,1)}), s8[2228224]{0:T(1024)(128)(4,1)S(1)}, s32[]{:S(2)}) async-start(s8[6422528]{0:T(1024)(128)(4,1)} %bitcast.31), calls=%async_computation.14 | async-start | bytes 4456448
  361.0 5.5 slice-start.3
  370.1 134.3 %all-gather.10.cloned.1.call-start = ((), (), s32[]{:S(2)}) async-start(), calls=%async_computation.7 | async-start | bytes 2064384 | tf_op jit(solution)/shard_map/all_gather | solution.py:85
  459.7 143.3 %all-gather.14.cloned.1.call-start = ((), (), s32[]{:S(2)}) async-start(), calls=%async_computation.9 | async-start | bytes 10485760 | tf_op jit(solution)/shard_map/all_gather | solution.py:95
  460.4 191.0 %all-gather.12.cloned.1.call-start = ((), (), s32[]{:S(2)}) async-start(), calls=%async_computation.8 | async-start | bytes 10485760 | tf_op jit(solution)/shard_map/all_gather | solution.py:96
  504.5 18.4 %copy-start.1 = (bf16[256,3584]{0,1:T(8,128)(2,1)S(1)}, bf16[256,3584]{0,1:T(8,128)(2,1)}, u32[]{:S(2)}) copy-start(bf16[256,3584]{0,1:T(8,128)(2,1)} %all-gather.6.cloned.1.call-done) | copy-start | bytes 5505028
  569.0 31.6 %all-to-all-start.1 = ((bf16[256,4,896]{0,2,1:T(8,128)(2,1)}), bf16[256,4,896]{0,2,1:T(8,128)(2,1)S(1)}, u32[]{:S(2)}, u32[]{:S(2)}) async-start(bf16[256,4,896]{0,2,1:T(8,128)(2,1)} %bitcast.36), calls=%async_computation.1 | async-start | bytes 3670016 | tf_op jit(solution)/shard_map/all_to_all | solution.py:92
  603.0 48.5 %copy-start.2 = (bf16[4,256,896]{2,1,0:T(8,128)(2,1)S(1)}, bf16[4,256,896]{2,1,0:T(8,128)(2,1)}, u32[]{:S(2)}) copy-start(bf16[4,256,896]{2,1,0:T(8,128)(2,1)} %copy.34) | copy-start | bytes 5505028
Sparse Core Ops, SparseCore 0:
  10.6 49.1 all-gather.5
  90.6 94.5 all-reduce.1
  201.5 66.1 reduce-scatter.6
  309.4 45.9 all-gather.7
  370.3 65.1 reduce-scatter.8
  459.8 44.6 all-gather.9
  506.0 81.8 all-gather.13
  590.1 61.2 all-gather.11
where the time goes:
time: 671 us; the launch traced here: 670 us
  waiting for transfers between devices  422 us (63%)
  matrix products  103 us (15%)
  blocking collectives  102 us (15%)
  between operations  14.4 us (2%)
  other arithmetic  13.9 us (2%)
  local copies, waits for them, and re-layouts  10.9 us (2%)
    unnamed x10, waiting for transfers between devices  131 us
    psum x1, waiting for transfers between devices, per_device(): lax.psum(partial_recon.astype(jnp.bfloat16), ('tensor', 'latent'))  94.5 us
    all_gather x1, waiting for transfers between devices, per_device(): lax.all_gather(centered_share, ('tensor', 'latent'), axis=1, tiled=True)  49.3 us
    all_to_all x1, blocking collectives, per_device(): lax.all_to_all(centered, 'batch', split_axis=1, concat_axis=0, tiled=True)  46.2 us
    all_gather x1, waiting for transfers between devices, per_device(): lax.all_gather(grad_share, ('tensor', 'latent'), axis=1, tiled=True)  45.8 us
    all_gather x1, waiting for transfers between devices, per_device(): lax.all_gather(recon_share, ('tensor', 'latent'), axis=1, tiled=True)  44 us
    all_gather x1, waiting for transfers between devices, per_device(): lax.all_gather(grad_preact, 'batch', axis=0, tiled=True)  33.3 us
    all_to_all x1, waiting for transfers between devices, per_device(): lax.all_to_all(grad_recon, 'batch', split_axis=1, concat_axis=0, tiled=True)  24.1 us
  transfers between devices with their start and end apart: 9, of which 8 were waited for; matrix products, arithmetic and copies ran while one was open for 6% of the time, Pallas kernels for 0%

commit v1 on v0

--- a/solution.py
+++ b/solution.py
@@ -1,9 +1,18 @@
+import functools
 import jax
 import jax.numpy as jnp
 from jax import lax
 from jax.sharding import PartitionSpec as P
 
 epsilon = 1e-06
+
+
+def move_scales(w_in, device_axis, lane_axis):
+    tile_out = lax.psum(lax.psum(w_in, axis_name=device_axis), axis_name=lane_axis)
+    return tile_out
+
+
+search_zones = functools.partial(move_scales, device_axis="latent", lane_axis="tensor")
 
 
 def per_device(
@@ -37,7 +46,7 @@
     )
     latents = jnp.maximum(preact, 0.0).astype(bf16)
     partial_recon = jnp.dot(latents, decoder_weight, preferred_element_type=f32)
-    recon_full = lax.psum(partial_recon.astype(jnp.bfloat16), ("tensor", "latent")).astype(
+    recon_full = search_zones(partial_recon.astype(jnp.bfloat16)).astype(
         jnp.float32
     ) + decoder_bias.astype(f32)
     scale_in = lax.rsqrt(

time: 671 us -> 712 us (1.061)
  waiting for transfers between devices: 422 us -> 462 us
    psum x1 -> x2, waiting for transfers between devices: 94.5 us -> 135 us  [the longest x1 76.4 us: move_scales(): lax.psum(w_in, axis_name=device_axis)]
    unnamed x10 -> x11, waiting for transfers between devices: 131 us -> 131 us
  transfers between devices with their start and end apart: 9 -> 10, of which waited for: 8 -> 9; matrix products, arithmetic and copies ran while one was open for 6% -> 6% of each run, Pallas kernels for 0% -> 0%
where the time goes in v1:
time: 712 us; the launch traced here: 711 us
  waiting for transfers between devices  462 us (65%)
  matrix products  103 us (14%)
  blocking collectives  102 us (14%)
  between operations  14.1 us (2%)
  other arithmetic  13.9 us (2%)
  local copies, waits for them, and re-layouts  10.9 us (2%)
    unnamed x11, waiting for transfers between devices  131 us
    psum x1, waiting for transfers between devices, move_scales(): lax.psum(w_in, axis_name=device_axis)  76.4 us
    psum x1, waiting for transfers between devices, move_scales(): lax.psum(lax.psum(w_in, axis_name=device_axis), axis_name=lane_axis)  58.3 us
    all_gather x1, waiting for transfers between devices, per_device(): lax.all_gather(centered_share, ('tensor', 'latent'), axis=1, tiled=True)  49.3 us
    all_to_all x1, blocking collectives, per_device(): lax.all_to_all(centered, 'batch', split_axis=1, concat_axis=0, tiled=True)  46.2 us
    all_gather x1, waiting for transfers between devices, per_device(): lax.all_gather(grad_share, ('tensor', 'latent'), axis=1, tiled=True)  45.8 us
    all_gather x1, waiting for transfers between devices, per_device(): lax.all_gather(recon_share, ('tensor', 'latent'), axis=1, tiled=True)  43.9 us
    all_gather x1, waiting for transfers between devices, per_device(): lax.all_gather(grad_preact, 'batch', axis=0, tiled=True)  33.3 us
  transfers between devices with their start and end apart: 10, of which 9 were waited for; matrix products, arithmetic and copies ran while one was open for 6% of the time, Pallas kernels for 0%

profile of v1, /device:TPU:0, one launch (start us, length us, event | category | flops | bytes accessed | tf_op | source)
XLA Modules:
  0.0 711.0 jit_solution(7854938726571878619)
XLA Ops:
  7.2 0.0 all-gather.6.cloned.1.call-start
  7.2 0.8 dynamic_slice.12
  8.0 1.8 subtract_convert_fusion
  9.7 0.0 all-gather.6.cloned.1.call-update
  9.8 0.0 all-reduce.3.cloned.1.call-start
  9.8 0.7 convert_element_type.74
  10.5 49.3 %all-gather.6.cloned.1.call-done = bf16[256,3584]{0,1:T(8,128)(2,1)} async-done(((bf16[256,448]{0,1:T(8,128)(2,1)}), bf16[256,3584]{0,1:T(8,128)(2,1)}) %all-gather.6.cloned.1.call-update) | async-done | bytes 1835024 | tf_op jit(solution)/shard_map/all_gather | solution.py:43
  59.8 15.2 %maximum_convert_fusion = (bf16[256,4096]{1,0:T(8,128)(2,1)S(1)}, f32[256,4096]{1,0:T(8,128)}) fusion(f32[4096]{0:T(1024)S(1)} %convert_element_type.74, bf16[256,3584]{0,1:T(8,128)(2,1)} %all-gather.6.cloned.1.call-done, bf16[3584,4096]{1,0:T(8,128)(2,1)} %param.13), kind=kOutput, calls=%fused_computation.11 | convolution fusion | flops 7519338496 | bytes 37502976 | tf_op jit(solution)/shard_map/dot_general | solution.py:44
  75.0 15.5 %convolution_convert_fusion.2 = bf16[256,3584]{1,0:T(8,128)(2,1)} fusion(bf16[256,4096]{1,0:T(8,128)(2,1)S(1)} %get-tuple-element.4, bf16[4096,3584]{1,0:T(8,128)(2,1)} %param.15), kind=kOutput, calls=%fused_computation.5 | convolution fusion | flops 7517110272 | bytes 33292288 | tf_op jit(solution)/shard_map/dot_general | solution.py:48
  90.4 0.0 all-reduce.3.cloned.1.call-update
  90.4 0.0 all-reduce.5.cloned.1.call-start
  90.5 76.4 %all-reduce.3.cloned.1.call-done = bf16[256,3584]{1,0:T(8,128)(2,1)} async-done(((bf16[256,3584]{1,0:T(8,128)(2,1)}), bf16[256,3584]{1,0:T(8,128)(2,1)}) %all-reduce.3.cloned.1.call-update) | async-done | bytes 1835024 | tf_op jit(solution)/shard_map/psum | solution.py:11
  166.9 0.0 all-reduce.5.cloned.1.call-update
  167.0 0.2 reduce-scatter.7.cloned.1.call-start
  167.2 58.3 %all-reduce.5.cloned.1.call-done = bf16[256,3584]{1,0:T(8,128)(2,1)} async-done(((bf16[256,3584]{1,0:T(8,128)(2,1)}), bf16[256,3584]{1,0:T(8,128)(2,1)}) %all-reduce.5.cloned.1.call-update) | async-done | bytes 1835024 | tf_op jit(solution)/shard_map/psum | solution.py:11
  225.5 4.0 convert_add_fusion
  229.5 5.6 fusion.30
  235.2 0.0 slice-start.5
  235.2 2.1 fusion.29
  237.4 4.3 fusion.2
  241.7 0.0 reduce-scatter.7.cloned.1.call-update
  241.7 0.0 all-gather.8.cloned.1.call-start
  241.8 0.1 copy.36
  241.9 0.8 broadcast_multiply_fusion
  242.7 0.8 dynamic-slice_convert_fusion
  243.4 65.0 %reduce-scatter.7.cloned.1.call-done = bf16[448,256]{1,0:T(8,128)(2,1)} async-done(((bf16[3584,256]{1,0:T(8,128)(2,1)}), bf16[448,256]{1,0:T(8,128)(2,1)}) %reduce-scatter.7.cloned.1.call-update) | async-done | bytes 229392
  308.5 1.1 copy.42
  309.6 0.1 fusion.20
  309.7 19.4 %psum.37 = f32[256]{0:T(256)S(1)} all-reduce(f32[256]{0:T(256)S(1)} %fusion.20), channel_id=1, replica_groups=mesh['batch'=4,'tensor'=2,'latent'=4] {'tensor','latent'}, use_global_device_ids=true, to_apply=%region_5.0 | all-reduce | flops 256 | bytes 2048 | tf_op jit(solution)/shard_map/psum | solution.py:65
  329.1 1.4 fusion.16
  330.6 17.2 %psum.38 = f32[256]{0:T(256)S(1)} all-reduce(f32[256]{0:T(256)S(1)} %fusion.16), channel_id=1, replica_groups=mesh['batch'=4,'tensor'=2,'latent'=4] {'tensor','latent'}, use_global_device_ids=true, to_apply=%region_7.0 | all-reduce | flops 256 | bytes 2048 | tf_op jit(solution)/shard_map/psum | solution.py:72
  347.8 1.4 fusion.19
  349.2 0.9 copy.37
  350.0 0.0 all-gather.8.cloned.1.call-update
  350.1 0.3 reduce-scatter.9.cloned.1.call-start
  350.3 45.8 %all-gather.8.cloned.1.call-done = bf16[256,3584]{0,1:T(8,128)(2,1)} async-done(((bf16[256,448]{0,1:T(8,128)(2,1)}), bf16[256,3584]{0,1:T(8,128)(2,1)}) %all-gather.8.cloned.1.call-update) | async-done | bytes 1835024 | tf_op jit(solution)/shard_map/all_gather | solution.py:75
  396.1 5.6 fusion.45
  401.8 0.0 slice-start.3
  401.8 5.5 fusion.21
  407.3 3.7 fusion.3
  410.9 0.0 reduce-scatter.9.cloned.1.call-update
  411.0 0.0 all-gather.10.cloned.1.call-start
  411.0 0.1 dynamic_slice.15
  411.1 65.4 %reduce-scatter.9.cloned.1.call-done = bf16[448,256]{1,0:T(8,128)(2,1)} async-done(((bf16[3584,256]{1,0:T(8,128)(2,1)}), bf16[448,256]{1,0:T(8,128)(2,1)}) %reduce-scatter.9.cloned.1.call-update) | async-done | bytes 229392
  476.5 1.1 copy.44
  477.6 1.4 multiply_reduce_fusion.1
  479.0 19.3 %psum.39 = f32[256]{0:T(256)S(1)} all-reduce(f32[256]{0:T(256)S(1)} %multiply_reduce_fusion.1), channel_id=1, replica_groups=mesh['batch'=4,'tensor'=2,'latent'=4] {'tensor','latent'}, use_global_device_ids=true, to_apply=%region_10.0 | all-reduce | flops 256 | bytes 2048 | tf_op jit(solution)/shard_map/psum | solution.py:92
  498.4 1.5 add_convert_fusion
  499.9 0.8 copy.39
  500.7 0.0 all-gather.10.cloned.1.call-update
  500.7 0.0 all-gather.14.cloned.1.call-start
  500.8 0.7 all-gather.14.cloned.1.call-update
  501.5 0.0 all-gather.12.cloned.1.call-start
  501.5 43.9 %all-gather.10.cloned.1.call-done = bf16[256,3584]{0,1:T(8,128)(2,1)} async-done(((bf16[256,448]{0,1:T(8,128)(2,1)}), bf16[256,3584]{0,1:T(8,128)(2,1)}) %all-gather.10.cloned.1.call-update) | async-done | bytes 1835024 | tf_op jit(solution)/shard_map/all_gather | solution.py:94
  545.5 18.3 %fusion = bf16[256,4096]{1,0:T(8,128)(2,1)} fusion(bf16[256,3584]{0,1:T(8,128)(2,1)} %all-gather.10.cloned.1.call-done, bf16[4096,3584]{1,0:T(8,128)(2,1)} %param.15, f32[256,4096]{1,0:T(8,128)} %get-tuple-element.5), kind=kOutput, calls=%fused_computation.6 | convolution fusion | flops 7519338496 | bytes 37486592 | tf_op jit(solution)/shard_map/dot_general | solution.py:95
  563.8 0.0 all-gather.12.cloned.1.call-update
  563.9 46.2 %all_to_all.38 = bf16[256,4,896]{0,2,1:T(8,128)(2,1)} all-to-all(bf16[256,4,896]{0,2,1:T(8,128)(2,1)S(1)} %bitcast.35), channel_id=1, replica_groups=mesh['batch'=4,'tensor'=2,'latent'=4] {'batch'}, dimensions={1} | all-to-all | bytes 3670016 | tf_op jit(solution)/shard_map/all_to_all | solution.py:100
  610.0 3.8 all-to-all-start.1
  613.9 3.6 copy.34
  617.5 24.1 %all-to-all-done.1 = bf16[256,4,896]{0,2,1:T(8,128)(2,1)S(1)} async-done(((bf16[256,4,896]{0,2,1:T(8,128)(2,1)}), bf16[256,4,896]{0,2,1:T(8,128)(2,1)S(1)}, u32[]{:S(2)}, u32[]{:S(2)}) %all-to-all-start.1) | async-done | bytes 1835040 | tf_op jit(solution)/shard_map/all_to_all | solution.py:101
  641.6 2.4 copy.40
  644.0 15.2 %convolution_convert_fusion = bf16[4096,896]{1,0:T(8,128)(2,1)} fusion(bf16[1024,4096]{1,0:T(8,128)(2,1)} %all-gather.14.cloned.1.call-done, bf16[1024,896]{1,0:T(8,128)(2,1)} %bitcast.38), kind=kOutput, calls=%fused_computation | convolution fusion | flops 7519862784 | bytes 17563648 | tf_op jit(solution)/shard_map/dot_general | solution.py:110
  659.1 33.3 %all-gather.12.cloned.1.call-done = bf16[1024,4096]{1,0:T(8,128)(2,1)} async-done(((bf16[256,4096]{1,0:T(8,128)(2,1)}), bf16[1024,4096]{1,0:T(8,128)(2,1)}) %all-gather.12.cloned.1.call-update) | async-done | bytes 8388624 | tf_op jit(solution)/shard_map/all_gather | solution.py:105
  692.4 12.1 %convolution_convert_fusion.1 = bf16[896,4096]{1,0:T(8,128)(2,1)} fusion(bf16[1024,896]{1,0:T(8,128)(2,1)S(1)} %bitcast.37, bf16[1024,4096]{1,0:T(8,128)(2,1)} %all-gather.12.cloned.1.call-done), kind=kOutput, calls=%fused_computation.1 | convolution fusion | flops 7519862784 | bytes 17563648 | tf_op jit(solution)/shard_map/dot_general | solution.py:107
  (34 shorter events, 0.1 us)
Async XLA Ops:
  7.2 52.6 %all-gather.6.cloned.1.call-start = ((), (), s32[]{:S(2)}) async-start(), calls=%async_computation.4 | async-start | bytes 2064384 | tf_op jit(solution)/shard_map/all_gather | solution.py:43
  9.8 157.2 %all-reduce.3.cloned.1.call-start = ((), (), s32[]{:S(2)}) async-start(), calls=%async_computation.5 | async-start | bytes 3670016 | tf_op jit(solution)/shard_map/psum | solution.py:11
  75.0 15.5 %copy-start = (bf16[256,4096]{1,0:T(8,128)(2,1)}, bf16[256,4096]{1,0:T(8,128)(2,1)S(1)}, u32[]{:S(2)}) copy-start(bf16[256,4096]{1,0:T(8,128)(2,1)S(1)} %get-tuple-element.4) | copy-start | bytes 6291460
  90.4 76.8 %copy-start.5 = (bf16[3584]{0:T(1024)(128)(2,1)S(1)}, bf16[3584]{0:T(1024)(128)(2,1)}, u32[]{:S(2)}) copy-start(bf16[3584]{0:T(1024)(128)(2,1)} %param.16) | copy-start | bytes 21508
  90.4 76.8 %copy-start.6 = (bf16[3584]{0:T(1024)(128)(2,1)S(1)}, bf16[3584]{0:T(1024)(128)(2,1)}, u32[]{:S(2)}) copy-start(bf16[3584]{0:T(1024)(128)(2,1)} %param.17) | copy-start | bytes 21508
  90.4 135.1 %all-reduce.5.cloned.1.call-start = ((), (), s32[]{:S(2)}) async-start(), calls=%async_computation.6 | async-start | bytes 3670016 | tf_op jit(solution)/shard_map/psum | solution.py:11
  167.0 141.5 %reduce-scatter.7.cloned.1.call-start = ((), (), s32[]{:S(2)}) async-start(), calls=%async_computation.11 | async-start | bytes 2064384
  225.5 9.6 %slice-start = ((s8[6422528]{0:T(1024)(128)(4,1)}), s8[4194304]{0:T(1024)(128)(4,1)S(1)}, s32[]{:S(2)}) async-start(s8[6422528]{0:T(1024)(128)(4,1)} %bitcast.29), calls=%async_computation.13 | async-start | bytes 8388608
  229.5 5.7 slice-start.1
  229.5 5.7 copy-start.3
  229.5 7.8 %slice-start.4 = ((s8[6422528]{0:T(1024)(128)(4,1)}), s8[4194304]{0:T(1024)(128)(4,1)S(1)}, s32[]{:S(2)}) async-start(s8[6422528]{0:T(1024)(128)(4,1)} %bitcast.41), calls=%async_computation.17 | async-start | bytes 8388608
  235.2 2.2 slice-start.5
  237.4 4.4 copy-start.4
  241.7 154.5 %all-gather.8.cloned.1.call-start = ((), (), s32[]{:S(2)}) async-start(), calls=%async_computation.7 | async-start | bytes 2064384 | tf_op jit(solution)/shard_map/all_gather | solution.py:75
  350.1 126.5 %reduce-scatter.9.cloned.1.call-start = ((), (), s32[]{:S(2)}) async-start(), calls=%async_computation.12 | async-start | bytes 2064384
  396.1 11.1 %slice-start.2 = ((s8[6422528]{0:T(1024)(128)(4,1)}), s8[2228224]{0:T(1024)(128)(4,1)S(1)}, s32[]{:S(2)}) async-start(s8[6422528]{0:T(1024)(128)(4,1)} %bitcast.31), calls=%async_computation.15 | async-start | bytes 4456448
  401.8 5.5 slice-start.3
  411.0 134.5 %all-gather.10.cloned.1.call-start = ((), (), s32[]{:S(2)}) async-start(), calls=%async_computation.8 | async-start | bytes 2064384 | tf_op jit(solution)/shard_map/all_gather | solution.py:94
  500.7 143.2 %all-gather.14.cloned.1.call-start = ((), (), s32[]{:S(2)}) async-start(), calls=%async_computation.10 | async-start | bytes 10485760 | tf_op jit(solution)/shard_map/all_gather | solution.py:104
  501.5 190.9 %all-gather.12.cloned.1.call-start = ((), (), s32[]{:S(2)}) async-start(), calls=%async_computation.9 | async-start | bytes 10485760 | tf_op jit(solution)/shard_map/all_gather | solution.py:105
  545.5 18.4 %copy-start.1 = (bf16[256,3584]{0,1:T(8,128)(2,1)S(1)}, bf16[256,3584]{0,1:T(8,128)(2,1)}, u32[]{:S(2)}) copy-start(bf16[256,3584]{0,1:T(8,128)(2,1)} %all-gather.6.cloned.1.call-done) | copy-start | bytes 5505028
  610.0 31.6 %all-to-all-start.1 = ((bf16[256,4,896]{0,2,1:T(8,128)(2,1)}), bf16[256,4,896]{0,2,1:T(8,128)(2,1)S(1)}, u32[]{:S(2)}, u32[]{:S(2)}) async-start(bf16[256,4,896]{0,2,1:T(8,128)(2,1)} %bitcast.36), calls=%async_computation.1 | async-start | bytes 3670016 | tf_op jit(solution)/shard_map/all_to_all | solution.py:101
  644.0 48.5 %copy-start.2 = (bf16[4,256,896]{2,1,0:T(8,128)(2,1)S(1)}, bf16[4,256,896]{2,1,0:T(8,128)(2,1)}, u32[]{:S(2)}) copy-start(bf16[4,256,896]{2,1,0:T(8,128)(2,1)} %copy.34) | copy-start | bytes 5505028
Sparse Core Ops, SparseCore 0:
  10.6 49.1 all-gather.5
  90.6 76.3 all-reduce.2
  169.2 56.2 all-reduce.4
  241.8 66.6 reduce-scatter.6
  350.2 45.9 all-gather.7
  411.1 65.4 reduce-scatter.8
  500.9 44.5 all-gather.9
  547.0 81.8 all-gather.13
  631.1 61.3 all-gather.11
